TPU v7x, 32 devices: a whole 2x2x4 slice. The times are simulated.
32 devices in a mesh: patch: 8 (over y, x, core), rhs: 4 (over z).
Axes of the slice: x: 2, y: 2, z: 4, core: 2. Of those that a mesh axis runs over, the one named last changes fastest.
Arguments:
- rhs_vectors: float32 [64, 16, 384], P('patch', 'rhs'), may hold values from -8 to 8
- near_blocks: bfloat16 [64, 4, 384, 384], P('patch'), may hold values from -1 to 5, as said below
- neighbours: int32 [64, 4], P('patch'), may hold values from 0 to 63, as said below
- up_maps: float32 [64, 64, 384], P('patch'), may hold values from -0.3125 to 0.3125
- shift_up: float32 [64, 64, 64], P('patch'), may hold values from -0.25 to 0.25
- far_lists: int32 [8, 4], P('patch'), may hold values from 0 to 7, as said below
- translations: float32 [8, 4, 64, 64], P('patch'), may hold values from -0.375 to 0.375
- shift_down: float32 [64, 64, 64], P('patch'), may hold values from -0.75 to 0.75
- down_maps: float32 [64, 384, 64], P('patch'), may hold values from -0.375 to 0.375
Outputs:
- solution: float32 [64, 16, 384], P('patch', 'rhs')
- residual: float32 [64, 16, 384], P('patch', 'rhs')
Inputs may be any that keep to these rules, and one draw needn't show every extreme that they name: `neighbours`: entry 0 of each row is the patch itself; every other entry names a patch of the same cell or of the cell just before or just after it, cyclically. `far_lists`: entry 0 of each row names the cell just before or just after the row's own cell, cyclically, and for cell 0 the cell just before it; every other entry names a cell other than the row's own. `near_blocks`: the blocks keep the operator's symmetric part positive definite.
All inputs are finite; a program needn't handle non-finite values.
Results may differ from a plain program's by a relative error of at most 0.008.
The roundings to bfloat16 on the way count: a program that leaves them out, or rounds other values in their place, can miss the bound.
Values may be sent and summed in bfloat16 or wider, within the bound.
A program may use at most 64 MiB of HBM per device.

v0:
```python
import jax
import jax.numpy as jnp
from jax import lax
from jax.sharding import PartitionSpec as P

ITERS = 2
HIGH = lax.Precision.HIGHEST


def with_halo(block, sides, width):
    for axis, dim in sides:
        count = lax.axis_size(axis)
        forward = [(i, i + 1) for i in range(count - 1)]
        forward.append((count - 1, 0))
        backward = [(target, source) for source, target in forward]
        low = lax.ppermute(
            lax.slice_in_dim(block, block.shape[dim] - width, None, axis=dim), axis, forward
        )
        high = lax.ppermute(lax.slice_in_dim(block, 0, width, axis=dim), axis, backward)
        block = jnp.concatenate([low, block, high], axis=dim)
    return block


def spd_solve(matrix, right):
    factor = jnp.linalg.cholesky(matrix)
    return jax.scipy.linalg.cho_solve((factor, True), right)


def gram(left, right):
    return jnp.einsum("pkw,plw->kl", left, right, precision=HIGH)


def mix(field, coeffs):
    return jnp.einsum("pkw,kl->plw", field, coeffs, precision=HIGH)


def residual_sum(residual):
    return lax.psum(gram(residual, residual), "patch")


def apply_operator(
    field,
    near_blocks,
    neighbours,
    up_maps,
    shift_up,
    far_lists,
    translations,
    shift_down,
    down_maps,
):
    patches = field.shape[0]
    count = lax.axis_size("patch")
    first = lax.axis_index("patch") * patches - patches
    rounded = field.astype(jnp.bfloat16)
    widened = with_halo(rounded, (("patch", 0),), patches)
    local_ids = jnp.mod(neighbours - first, patches * count)
    picked = widened[local_ids]
    near = jnp.einsum("pjvw,pjkw->pkv", near_blocks, picked, preferred_element_type=jnp.float32)
    moments = jnp.einsum("pew,pkw->pke", up_maps, field, precision=HIGH)
    cell_moment = jnp.einsum("pfe,pke->kf", shift_up, moments, precision=HIGH)
    sources = far_lists[0]
    table = translations[0]
    piece = lax.all_gather(cell_moment[None], "patch", axis=0, tiled=True)
    labels = jnp.arange(piece.shape[0], dtype=jnp.int32)
    select = (sources[:, None] == labels[None, :]).astype(jnp.float32)
    chosen = jnp.einsum("ji,ike->jke", select, piece, precision=HIGH)
    local_exp = jnp.zeros_like(cell_moment) + jnp.einsum(
        "jfe,jke->kf", table, chosen, precision=HIGH
    )
    patch_exp = jnp.einsum("pfe,ke->pkf", shift_down, local_exp, precision=HIGH)
    far = jnp.einsum("pvf,pkf->pkv", down_maps, patch_exp, precision=HIGH)
    return near + far


def on_device(
    rhs_vectors,
    near_blocks,
    neighbours,
    up_maps,
    shift_up,
    far_lists,
    translations,
    shift_down,
    down_maps,
):
    my_cols = rhs_vectors.shape[1]
    offset = lax.axis_index("rhs") * my_cols
    residual = lax.all_gather(rhs_vectors, "rhs", axis=1, tiled=True)
    solution = jnp.zeros_like(residual)
    direction = residual
    current = jnp.zeros((residual.shape[1], residual.shape[1]), jnp.float32)
    for step in range(ITERS):
        image = apply_operator(
            direction,
            near_blocks,
            neighbours,
            up_maps,
            shift_up,
            far_lists,
            translations,
            shift_down,
            down_maps,
        )
        if step == 0:
            current = residual_sum(residual)
        curve = lax.psum(gram(direction, image), "patch")
        curve = 0.5 * (curve + curve.T)
        alpha = spd_solve(curve, current)
        solution = solution + mix(direction, alpha)
        residual = residual - mix(image, alpha)
        if step + 1 < ITERS:
            following = residual_sum(residual)
            beta = spd_solve(current, following)
            direction = residual + mix(direction, beta)
            current = following
    solution_mine = lax.dynamic_slice_in_dim(solution, offset, my_cols, 1)
    residual_mine = lax.dynamic_slice_in_dim(residual, offset, my_cols, 1)
    return (solution_mine, residual_mine)


def solution(mesh):
    return jax.shard_map(
        on_device,
        mesh=mesh,
        in_specs=(
            P("patch", "rhs", None),
            P("patch", None, None, None),
            P("patch", None),
            P("patch", None, None),
            P("patch", None, None),
            P("patch", None),
            P("patch", None, None, None),
            P("patch", None, None),
            P("patch", None, None),
        ),
        out_specs=(P("patch", "rhs", None), P("patch", "rhs", None)),
        check_vma=False,
    )
```

profile of v0, /device:TPU:0, one launch (start us, length us, event | category | flops | bytes accessed | tf_op | source)
XLA Modules:
  0.0 129.5 jit_solution(5300560113778208520)
XLA Ops:
  0.6 0.9 copy.61
  1.5 15.5 %all_gather.9 = f32[8,16,384]{2,0,1:T(8,128)S(1)} all-gather(f32[8,4,384]{2,0,1:T(8,128)S(1)} %copy.61), channel_id=1, replica_groups=mesh['patch'=8,'rhs'=4] {'rhs'}, dimensions={1}, use_global_device_ids=true | all-gather | bytes 245760 | tf_op jit(solution)/shard_map/all_gather | solution.py:89
  17.0 0.1 collective-permute-start.1
  17.1 0.5 collective-permute-start
  17.6 0.4 convolution_bitcast_fusion.14
  17.9 0.7 compare_select_fusion
  18.7 0.1 copy.63
  18.7 0.1 reshape.17
  18.8 2.1 %fusion.11 = f32[8,16,64]{2,1,0:T(8,128)S(1)} fusion(f32[8,64,384]{2,1,0:T(8,128)} %param.15, f32[8,16,384]{2,0,1:T(8,128)S(1)} %all_gather.9), kind=kOutput, calls=%fused_computation.33 | convolution fusion | flops 37748736 | bytes 1015808 | tf_op jit(solution)/shard_map/pew,pkw->pke/dot_general | solution.py:60
  20.9 1.2 convolution_bitcast_fusion.11
  22.1 9.3 %all-gather = f32[128,64]{1,0:T(8,128)S(1)} all-gather(f32[16,64]{1,0:T(8,128)S(1)} %convolution_bitcast_fusion.11), channel_id=2, replica_groups=mesh['patch'=8,'rhs'=4] {'patch'}, dimensions={0}, use_global_device_ids=true | all-gather | bytes 36864 | tf_op jit(solution)/shard_map/all_gather | solution.py:64
  31.4 0.9 fusion.15
  32.3 1.1 fusion.4
  33.4 1.7 %convolution_bitcast_fusion.6 = f32[8,16,64]{2,1,0:T(8,128)S(1)} fusion(f32[16,64,1]{1,0,2:T(8,128)S(1)} %fusion.4, f32[8,64,64]{2,1,0:T(8,128)} %param.19), kind=kOutput, calls=%fused_computation.12 | convolution fusion | flops 6291456 | bytes 167936 | tf_op jit(solution)/shard_map/pfe,ke->pkf/dot_general | solution.py:71
  35.2 0.6 gather_fusion
  35.9 6.3 %convolution_bitcast_fusion.4 = f32[8,16,384]{2,1,0:T(8,128)S(1)} fusion(bf16[8,4,16,384]{3,2,1,0:T(8,128)(2,1)S(1)} %bitcast.140, bf16[8,4,384,384]{3,2,1,0:T(8,128)(2,1)} %param.13), kind=kOutput, calls=%fused_computation.10 | convolution fusion | flops 150994944 | bytes 10027008 | tf_op jit(solution)/shard_map/pjvw,pjkw->pkv/dot_general | solution.py:59
  42.2 0.6 convolution_add_fusion.1
  42.8 0.4 convolution_bitcast_fusion.15
  43.2 23.6 %all-reduce = (f32[16,16]{0,1:T(8,128)S(1)}, f32[16,16]{1,0:T(8,128)S(1)}) all-reduce(f32[16,16]{0,1:T(8,128)S(1)} %convolution_bitcast_fusion.14, f32[16,16]{1,0:T(8,128)S(1)} %convolution_bitcast_fusion.15), channel_id=1, replica_groups=mesh['patch'=8,'rhs'=4] {'patch'}, use_global_device_ids=true, to_apply=%region_3.5 | all-reduce | flops 512 | bytes 4096 | tf_op jit(solution)/shard_map/psum | solution.py:38
  66.8 0.1 copy.69
  66.9 0.1 copy.70
  67.0 1.5 %cholesky.59 = f32[16,16]{1,0:T(8,128)S(1)} custom-call(f32[16,16]{1,0:T(8,128)S(1)} %fusion.35), custom_call_target="Cholesky" | custom-call | tf_op jit(solution)/shard_map/jit(cholesky)/cholesky | solution.py:25
  68.4 0.6 compare_reduce_fusion.2
  69.1 0.6 fusion.20
  69.8 1.2 custom-call.9
  71.0 0.1 copy.78
  71.0 0.2 fusion.33
  71.3 0.2 convolution_bitcast_fusion.10
  71.5 0.3 fusion.1
  71.8 0.3 convolution_bitcast_fusion.13
  72.1 12.1 %psum.30 = f32[16,16]{1,0:T(8,128)S(1)} all-reduce(f32[16,16]{1,0:T(8,128)S(1)} %convolution_bitcast_fusion.13), channel_id=1, replica_groups=mesh['patch'=8,'rhs'=4] {'patch'}, use_global_device_ids=true, to_apply=%region_4.7 | all-reduce | flops 256 | bytes 2048 | tf_op jit(solution)/shard_map/psum | solution.py:38
  84.2 1.4 %cholesky.70 = f32[16,16]{1,0:T(8,128)S(1)} custom-call(f32[16,16]{1,0:T(8,128)S(1)} %fusion.31), custom_call_target="Cholesky" | custom-call | tf_op jit(solution)/shard_map/jit(cholesky)/cholesky | solution.py:25
  85.7 0.6 compare_reduce_fusion.1
  86.3 0.6 fusion.21
  87.0 1.2 custom-call.10
  88.2 0.2 fusion.29
  88.4 0.2 convolution_bitcast_fusion.9
  88.6 0.3 fusion.43
  89.0 0.1 collective-permute-start.3
  89.0 0.5 collective-permute-start.2
  89.5 0.3 fusion.7
  89.8 0.9 fusion.44
  90.8 0.3 convolution_bitcast_fusion.8
  91.1 9.4 %all-gather.1 = f32[128,64]{1,0:T(8,128)S(1)} all-gather(f32[16,64]{1,0:T(8,128)S(1)} %convolution_bitcast_fusion.8), channel_id=3, replica_groups=mesh['patch'=8,'rhs'=4] {'patch'}, dimensions={0}, use_global_device_ids=true | all-gather | bytes 36864 | tf_op jit(solution)/shard_map/all_gather | solution.py:64
  100.4 0.2 fusion.13
  100.7 0.2 fusion.2
  100.9 0.7 convolution_bitcast_fusion.5
  101.7 0.6 gather_fusion.1
  102.3 6.2 %convolution_bitcast_fusion.3 = f32[8,16,384]{2,1,0:T(8,128)S(1)} fusion(bf16[8,4,16,384]{3,2,1,0:T(8,128)(2,1)S(1)} %bitcast.139, bf16[8,4,384,384]{3,2,1,0:T(8,128)(2,1)} %param.13), kind=kOutput, calls=%fused_computation.9 | convolution fusion | flops 150994944 | bytes 10027008 | tf_op jit(solution)/shard_map/pjvw,pjkw->pkv/dot_general | solution.py:59
  108.5 0.6 convolution_add_fusion
  109.2 0.3 convolution_bitcast_fusion.12
  109.5 13.5 %psum.31 = f32[16,16]{1,0:T(8,128)S(1)} all-reduce(f32[16,16]{1,0:T(8,128)S(1)} %convolution_bitcast_fusion.12), channel_id=1, replica_groups=mesh['patch'=8,'rhs'=4] {'patch'}, use_global_device_ids=true, to_apply=%region_5.8 | all-reduce | flops 256 | bytes 2048 | tf_op jit(solution)/shard_map/psum | solution.py:107
  123.0 0.1 copy.83
  123.0 0.1 copy.84
  123.1 1.5 %cholesky.81 = f32[16,16]{1,0:T(8,128)S(1)} custom-call(f32[16,16]{1,0:T(8,128)S(1)} %fusion.26), custom_call_target="Cholesky" | custom-call | tf_op jit(solution)/shard_map/jit(cholesky)/cholesky | solution.py:25
  124.6 0.6 compare_reduce_fusion
  125.3 0.6 fusion.22
  125.9 1.2 custom-call.11
  127.1 0.2 fusion.24
  127.3 0.2 convolution_bitcast_fusion.7
  127.6 0.3 fusion.45
  127.9 0.3 convolution_bitcast_fusion
  128.2 0.6 dynamic-slice_subtract_fusion
  128.8 0.6 fusion.17
  (28 shorter events, 0.4 us)
Async XLA Ops:
  0.6 41.6 %copy-start = (f32[8,384,64]{1,2,0:T(8,128)S(1)}, f32[8,384,64]{1,2,0:T(8,128)}, u32[]{:S(2)}) copy-start(f32[8,384,64]{1,2,0:T(8,128)} %param.20) | copy-start | bytes 2359300
  17.0 18.1 %collective-permute-start.1 = (bf16[8,16,384]{2,1,0:T(8,128)(2,1)S(1)}, bf16[8,16,384]{2,1,0:T(8,128)(2,1)S(1)}, u32[]{:S(2)}, u32[]{:S(2)}) collective-permute-start(bf16[8,16,384]{2,1,0:T(8,128)(2,1)S(1)} %copy.116), channel_id=1, source_target_pairs={{4,0},{8,4},{12,8},{16,12},{20,16},{24,20},{28,24},{0,28},{5,1},{9... | collective-permute-start | bytes 294920 | tf_op jit(solution)/shard_map/ppermute | solution.py:19
  17.1 18.1 %collective-permute-start = (bf16[8,16,384]{2,1,0:T(8,128)(2,1)S(1)}, bf16[8,16,384]{2,1,0:T(8,128)(2,1)S(1)}, u32[]{:S(2)}, u32[]{:S(2)}) collective-permute-start(bf16[8,16,384]{2,1,0:T(8,128)(2,1)S(1)} %copy.116), channel_id=1, source_target_pairs={{0,4},{4,8},{8,12},{12,16},{16,20},{20,24},{24,28},{28,0},{1,5},{5... | collective-permute-start | bytes 294920 | tf_op jit(solution)/shard_map/ppermute | solution.py:16
  35.8 54.0 %copy-start.1 = (f32[8,64,384]{2,1,0:T(8,128)S(1)}, f32[8,64,384]{2,1,0:T(8,128)}, u32[]{:S(2)}) copy-start(f32[8,64,384]{2,1,0:T(8,128)} %param.15) | copy-start | bytes 2359300
  35.9 54.9 %copy-start.2 = (f32[8,64,64]{2,1,0:T(8,128)S(1)}, f32[8,64,64]{2,1,0:T(8,128)}, u32[]{:S(2)}) copy-start(f32[8,64,64]{2,1,0:T(8,128)} %param.16) | copy-start | bytes 393220
  35.9 64.6 %copy-start.5 = (s32[1,4]{1,0:T(1,128)S(1)}, s32[1,4]{1,0:T(1,128)}, u32[]{:S(2)}) copy-start(s32[1,4]{1,0:T(1,128)} %param.17) | copy-start | bytes 52
  35.9 64.8 %copy-start.4 = (f32[1,4,64,64]{3,2,1,0:T(8,128)S(1)}, f32[1,4,64,64]{3,2,1,0:T(8,128)}, u32[]{:S(2)}) copy-start(f32[1,4,64,64]{3,2,1,0:T(8,128)} %param.18) | copy-start | bytes 196612
  35.9 65.0 %copy-start.3 = (f32[8,64,64]{2,1,0:T(8,128)S(1)}, f32[8,64,64]{2,1,0:T(8,128)}, u32[]{:S(2)}) copy-start(f32[8,64,64]{2,1,0:T(8,128)} %param.19) | copy-start | bytes 393220
  89.0 12.6 %collective-permute-start.3 = (bf16[8,16,384]{2,1,0:T(8,128)(2,1)S(1)}, bf16[8,16,384]{2,1,0:T(8,128)(2,1)S(1)}, u32[]{:S(2)}, u32[]{:S(2)}) collective-permute-start(bf16[8,16,384]{2,1,0:T(8,128)(2,1)S(1)} %get-tuple-element.6), channel_id=1, source_target_pairs={{4,0},{8,4},{12,8},{16,12},{20,16},{24,20},{28,24},{0,28},{5,1},{9... | collective-permute-start | bytes 294920 | tf_op jit(solution)/shard_map/ppermute | solution.py:19
  89.0 12.6 %collective-permute-start.2 = (bf16[8,16,384]{2,1,0:T(8,128)(2,1)S(1)}, bf16[8,16,384]{2,1,0:T(8,128)(2,1)S(1)}, u32[]{:S(2)}, u32[]{:S(2)}) collective-permute-start(bf16[8,16,384]{2,1,0:T(8,128)(2,1)S(1)} %get-tuple-element.6), channel_id=1, source_target_pairs={{0,4},{4,8},{8,12},{12,16},{16,20},{20,24},{24,28},{28,0},{1,5},{5... | collective-permute-start | bytes 294920 | tf_op jit(solution)/shard_map/ppermute | solution.py:16
where the time goes:
time: 130 us; the launch traced here: 129 us
  blocking collectives  83.3 us (64%)
  matrix products  27.2 us (21%)
  other arithmetic  14.2 us (11%)
  local copies, waits for them, and re-layouts  2.76 us (2%)
    psum x2, blocking collectives, residual_sum(): return lax.psum(gram(residual, residual), 'patch')  35.7 us
    all_gather x2, blocking collectives, apply_operator(): piece = lax.all_gather(cell_moment[None], 'patch', axis=0, tiled=True)  18.7 us
    all_gather x1, blocking collectives, on_device(): residual = lax.all_gather(rhs_vectors, 'rhs', axis=1, tiled=True)  15.5 us
    psum x1, blocking collectives, on_device(): curve = lax.psum(gram(direction, image), 'patch')  13.5 us
    dot_general x2, matrix products, apply_operator(): jnp.einsum('pjvw,pjkw->pkv', near_blocks, picked, preferred_element_type=...  12.5 us
    another operation x9, other arithmetic, spd_solve(): factor = jnp.linalg.cholesky(matrix)  6.39 us
    another operation x6, other arithmetic, spd_solve(): return jax.scipy.linalg.cho_solve((factor, True), right)  5.63 us
    dot_general x2, matrix products, apply_operator(): moments = jnp.einsum('pew,pkw->pke', up_maps, field, precision=HIGH)  2.99 us
  transfers between devices with their start and end apart: 4, of which 0 were waited for; matrix products, arithmetic and copies ran while one was open for 8% of the time, Pallas kernels for 0%

commit v1 on v0

--- a/solution.py
+++ b/solution.py
@@ -5,6 +5,11 @@
 
 ITERS = 2
 HIGH = lax.Precision.HIGHEST
+
+
+def add_all(x, mesh_axis):
+    parts = lax.all_gather(x, mesh_axis)
+    return jnp.sum(parts, axis=0)
 
 
 def with_halo(block, sides, width):
@@ -35,7 +40,7 @@
 
 
 def residual_sum(residual):
-    return lax.psum(gram(residual, residual), "patch")
+    return add_all(gram(residual, residual), "patch")
 
 
 def apply_operator(

time: 130 us -> 126 us (0.969)
  blocking collectives: 83.3 us -> 78.8 us
    psum x2 -> x0, blocking collectives: 35.7 us -> none  [residual_sum(): return lax.psum(gram(residual, residual), 'patch')]
    all_gather x0 -> x2, blocking collectives: none -> 17.6 us  [add_all(): parts = lax.all_gather(x, mesh_axis)]
    psum x1 -> x2, blocking collectives: 13.5 us -> 27 us  [on_device(): curve = lax.psum(gram(direction, image), 'patch')]
    ppermute x2, starting transfers between devices: 0.12 us -> 1.52 us  [with_halo(): lax.ppermute(lax.slice_in_dim(block, 0, width, axis=dim), axis, backward)]
  transfers between devices with their start and end apart: 4 -> 4, of which waited for: 0 -> 0; matrix products, arithmetic and copies ran while one was open for 8% -> 12% of each run, Pallas kernels for 0% -> 0%
where the time goes in v1:
time: 126 us
  blocking collectives  78.8 us (63%)
  matrix products  27.2 us (22%)
  other arithmetic  14.2 us (11%)
  local copies, waits for them, and re-layouts  2.76 us (2%)
  starting transfers between devices  2.02 us (2%)
    psum x2, blocking collectives, on_device(): curve = lax.psum(gram(direction, image), 'patch')  27 us
    all_gather x2, blocking collectives, apply_operator(): piece = lax.all_gather(cell_moment[None], 'patch', axis=0, tiled=True)  18.8 us
    all_gather x2, blocking collectives, add_all(): parts = lax.all_gather(x, mesh_axis)  17.6 us
    all_gather x1, blocking collectives, on_device(): residual = lax.all_gather(rhs_vectors, 'rhs', axis=1, tiled=True)  15.5 us
    dot_general x2, matrix products, apply_operator(): jnp.einsum('pjvw,pjkw->pkv', near_blocks, picked, preferred_element_type=...  12.5 us
    another operation x9, other arithmetic, spd_solve(): factor = jnp.linalg.cholesky(matrix)  6.39 us
    another operation x6, other arithmetic, spd_solve(): return jax.scipy.linalg.cho_solve((factor, True), right)  5.63 us
    dot_general x2, matrix products, apply_operator(): moments = jnp.einsum('pew,pkw->pke', up_maps, field, precision=HIGH)  2.99 us
  transfers between devices with their start and end apart: 4, of which 0 were waited for; matrix products, arithmetic and copies ran while one was open for 12% of the time, Pallas kernels for 0%

profile of v1, /device:TPU:0, one launch (start us, length us, event | category | flops | bytes accessed | tf_op | source)
XLA Modules:
  0.0 125.9 jit_solution(17562090675996968210)
XLA Ops:
  0.6 0.9 copy.58
  1.5 15.5 %all_gather.21 = f32[8,16,384]{2,0,1:T(8,128)S(1)} all-gather(f32[8,4,384]{2,0,1:T(8,128)S(1)} %copy.58), channel_id=1, replica_groups=mesh['patch'=8,'rhs'=4] {'rhs'}, dimensions={1}, use_global_device_ids=true | all-gather | bytes 245760 | tf_op jit(solution)/shard_map/all_gather | solution.py:94
  17.0 0.1 collective-permute-start.1
  17.1 0.5 collective-permute-start
  17.6 0.3 convolution_bitcast_fusion.14
  17.9 9.3 %all-gather.1 = f32[128,16]{1,0:T(8,128)S(1)} all-gather(f32[16,16]{1,0:T(8,128)S(1)} %convolution_bitcast_fusion.14), channel_id=3, replica_groups=mesh['patch'=8,'rhs'=4] {'patch'}, dimensions={0}, use_global_device_ids=true | all-gather | bytes 9216 | tf_op jit(solution)/shard_map/all_gather | solution.py:11
  27.2 0.7 compare_select_fusion
  27.9 0.1 copy.60
  28.0 0.1 reshape.17
  28.1 2.1 %fusion.11 = f32[8,16,64]{2,1,0:T(8,128)S(1)} fusion(f32[8,64,384]{2,1,0:T(8,128)} %param.15, f32[8,16,384]{2,0,1:T(8,128)S(1)} %all_gather.21), kind=kOutput, calls=%fused_computation.33 | convolution fusion | flops 37748736 | bytes 1015808 | tf_op jit(solution)/shard_map/pew,pkw->pke/dot_general | solution.py:65
  30.1 1.2 convolution_bitcast_fusion.11
  31.4 9.3 %all-gather = f32[128,64]{1,0:T(8,128)S(1)} all-gather(f32[16,64]{1,0:T(8,128)S(1)} %convolution_bitcast_fusion.11), channel_id=2, replica_groups=mesh['patch'=8,'rhs'=4] {'patch'}, dimensions={0}, use_global_device_ids=true | all-gather | bytes 36864 | tf_op jit(solution)/shard_map/all_gather | solution.py:69
  40.6 0.1 copy.74
  40.7 1.5 %cholesky.70 = f32[16,16]{1,0:T(8,128)S(1)} custom-call(f32[16,16]{1,0:T(8,128)S(1)} %fusion.31), custom_call_target="Cholesky" | custom-call | tf_op jit(solution)/shard_map/jit(cholesky)/cholesky | solution.py:30
  42.2 0.6 compare_reduce_fusion.1
  42.8 0.6 fusion.21
  43.5 1.2 custom-call.10
  44.7 0.9 fusion.15
  45.6 1.1 fusion.4
  46.7 1.7 %convolution_bitcast_fusion.6 = f32[8,16,64]{2,1,0:T(8,128)S(1)} fusion(f32[16,64,1]{1,0,2:T(8,128)S(1)} %fusion.4, f32[8,64,64]{2,1,0:T(8,128)} %param.19), kind=kOutput, calls=%fused_computation.12 | convolution fusion | flops 6291456 | bytes 167936 | tf_op jit(solution)/shard_map/pfe,ke->pkf/dot_general | solution.py:76
  48.5 0.6 gather_fusion
  49.2 6.3 %convolution_bitcast_fusion.4 = f32[8,16,384]{2,1,0:T(8,128)S(1)} fusion(bf16[8,4,16,384]{3,2,1,0:T(8,128)(2,1)S(1)} %bitcast.142, bf16[8,4,384,384]{3,2,1,0:T(8,128)(2,1)} %param.13), kind=kOutput, calls=%fused_computation.10 | convolution fusion | flops 150994944 | bytes 10027008 | tf_op jit(solution)/shard_map/pjvw,pjkw->pkv/dot_general | solution.py:64
  55.5 0.6 convolution_add_fusion.1
  56.1 0.4 convolution_bitcast_fusion.15
  56.5 13.5 %psum.14 = f32[16,16]{1,0:T(8,128)S(1)} all-reduce(f32[16,16]{1,0:T(8,128)S(1)} %convolution_bitcast_fusion.15), channel_id=1, replica_groups=mesh['patch'=8,'rhs'=4] {'patch'}, use_global_device_ids=true, to_apply=%region_0.1 | all-reduce | flops 256 | bytes 2048 | tf_op jit(solution)/shard_map/psum | solution.py:112
  70.0 0.1 copy.66
  70.1 0.1 copy.67
  70.1 1.5 %cholesky.59 = f32[16,16]{1,0:T(8,128)S(1)} custom-call(f32[16,16]{1,0:T(8,128)S(1)} %fusion.35), custom_call_target="Cholesky" | custom-call | tf_op jit(solution)/shard_map/jit(cholesky)/cholesky | solution.py:30
  71.6 0.6 compare_reduce_fusion.2
  72.3 0.6 fusion.20
  72.9 1.2 custom-call.9
  74.2 0.2 fusion.33
  74.4 0.2 convolution_bitcast_fusion.10
  74.6 0.3 fusion.1
  74.9 0.3 convolution_bitcast_fusion.13
  75.2 8.3 %all-gather.2 = f32[128,16]{1,0:T(8,128)S(1)} all-gather(f32[16,16]{1,0:T(8,128)S(1)} %convolution_bitcast_fusion.13), channel_id=4, replica_groups=mesh['patch'=8,'rhs'=4] {'patch'}, dimensions={0}, use_global_device_ids=true | all-gather | bytes 9216 | tf_op jit(solution)/shard_map/all_gather | solution.py:11
  83.6 0.2 fusion.29
  83.8 0.2 convolution_bitcast_fusion.9
  84.0 0.3 fusion.43
  84.3 1.5 %collective-permute-start.3 = (bf16[8,16,384]{2,1,0:T(8,128)(2,1)S(1)}, bf16[8,16,384]{2,1,0:T(8,128)(2,1)S(1)}, u32[]{:S(2)}, u32[]{:S(2)}) collective-permute-start(bf16[8,16,384]{2,1,0:T(8,128)(2,1)S(1)} %get-tuple-element.4), channel_id=1, source_target_pairs={{4,0},{8,4},{12,8},{16,12},{20,16},{24,20},{28,24},{0,28},{5,1},{9... | collective-permute-start | bytes 294920 | tf_op jit(solution)/shard_map/ppermute | solution.py:24
  85.7 0.3 fusion.7
  86.1 0.9 fusion.44
  87.0 0.3 convolution_bitcast_fusion.8
  87.3 9.5 %all-gather.3 = f32[128,64]{1,0:T(8,128)S(1)} all-gather(f32[16,64]{1,0:T(8,128)S(1)} %convolution_bitcast_fusion.8), channel_id=5, replica_groups=mesh['patch'=8,'rhs'=4] {'patch'}, dimensions={0}, use_global_device_ids=true | all-gather | bytes 36864 | tf_op jit(solution)/shard_map/all_gather | solution.py:69
  96.8 0.2 fusion.13
  97.0 0.2 fusion.2
  97.2 0.7 convolution_bitcast_fusion.5
  98.1 0.6 gather_fusion.1
  98.7 6.2 %convolution_bitcast_fusion.3 = f32[8,16,384]{2,1,0:T(8,128)S(1)} fusion(bf16[8,4,16,384]{3,2,1,0:T(8,128)(2,1)S(1)} %bitcast.141, bf16[8,4,384,384]{3,2,1,0:T(8,128)(2,1)} %param.13), kind=kOutput, calls=%fused_computation.9 | convolution fusion | flops 150994944 | bytes 10027008 | tf_op jit(solution)/shard_map/pjvw,pjkw->pkv/dot_general | solution.py:64
  104.9 0.6 convolution_add_fusion
  105.5 0.3 convolution_bitcast_fusion.12
  105.9 13.5 %psum.15 = f32[16,16]{1,0:T(8,128)S(1)} all-reduce(f32[16,16]{1,0:T(8,128)S(1)} %convolution_bitcast_fusion.12), channel_id=1, replica_groups=mesh['patch'=8,'rhs'=4] {'patch'}, use_global_device_ids=true, to_apply=%region_5.8 | all-reduce | flops 256 | bytes 2048 | tf_op jit(solution)/shard_map/psum | solution.py:112
  119.4 0.1 copy.79
  119.4 0.1 copy.80
  119.5 1.5 %cholesky.81 = f32[16,16]{1,0:T(8,128)S(1)} custom-call(f32[16,16]{1,0:T(8,128)S(1)} %fusion.26), custom_call_target="Cholesky" | custom-call | tf_op jit(solution)/shard_map/jit(cholesky)/cholesky | solution.py:30
  121.0 0.6 compare_reduce_fusion
  121.7 0.6 fusion.22
  122.3 1.2 custom-call.11
  123.5 0.2 fusion.24
  123.7 0.2 convolution_bitcast_fusion.7
  123.9 0.3 fusion.45
  124.3 0.3 convolution_bitcast_fusion
  124.6 0.6 dynamic-slice_subtract_fusion
  125.2 0.6 fusion.17
  (31 shorter events, 0.4 us)
Async XLA Ops:
  0.6 54.9 %copy-start = (f32[8,384,64]{1,2,0:T(8,128)S(1)}, f32[8,384,64]{1,2,0:T(8,128)}, u32[]{:S(2)}) copy-start(f32[8,384,64]{1,2,0:T(8,128)} %param.20) | copy-start | bytes 2359300
  17.0 31.4 %collective-permute-start.1 = (bf16[8,16,384]{2,1,0:T(8,128)(2,1)S(1)}, bf16[8,16,384]{2,1,0:T(8,128)(2,1)S(1)}, u32[]{:S(2)}, u32[]{:S(2)}) collective-permute-start(bf16[8,16,384]{2,1,0:T(8,128)(2,1)S(1)} %copy.110), channel_id=1, source_target_pairs={{4,0},{8,4},{12,8},{16,12},{20,16},{24,20},{28,24},{0,28},{5,1},{9... | collective-permute-start | bytes 294920 | tf_op jit(solution)/shard_map/ppermute | solution.py:24
  17.1 31.4 %collective-permute-start = (bf16[8,16,384]{2,1,0:T(8,128)(2,1)S(1)}, bf16[8,16,384]{2,1,0:T(8,128)(2,1)S(1)}, u32[]{:S(2)}, u32[]{:S(2)}) collective-permute-start(bf16[8,16,384]{2,1,0:T(8,128)(2,1)S(1)} %copy.110), channel_id=1, source_target_pairs={{0,4},{4,8},{8,12},{12,16},{16,20},{20,24},{24,28},{28,0},{1,5},{5... | collective-permute-start | bytes 294920 | tf_op jit(solution)/shard_map/ppermute | solution.py:21
  49.1 36.9 %copy-start.1 = (f32[8,64,384]{2,1,0:T(8,128)S(1)}, f32[8,64,384]{2,1,0:T(8,128)}, u32[]{:S(2)}) copy-start(f32[8,64,384]{2,1,0:T(8,128)} %param.15) | copy-start | bytes 2359300
  49.2 37.8 %copy-start.2 = (f32[8,64,64]{2,1,0:T(8,128)S(1)}, f32[8,64,64]{2,1,0:T(8,128)}, u32[]{:S(2)}) copy-start(f32[8,64,64]{2,1,0:T(8,128)} %param.16) | copy-start | bytes 393220
  49.2 47.6 %copy-start.5 = (s32[1,4]{1,0:T(1,128)S(1)}, s32[1,4]{1,0:T(1,128)}, u32[]{:S(2)}) copy-start(s32[1,4]{1,0:T(1,128)} %param.17) | copy-start | bytes 52
  49.2 47.8 %copy-start.4 = (f32[1,4,64,64]{3,2,1,0:T(8,128)S(1)}, f32[1,4,64,64]{3,2,1,0:T(8,128)}, u32[]{:S(2)}) copy-start(f32[1,4,64,64]{3,2,1,0:T(8,128)} %param.18) | copy-start | bytes 196612
  49.2 48.0 %copy-start.3 = (f32[8,64,64]{2,1,0:T(8,128)S(1)}, f32[8,64,64]{2,1,0:T(8,128)}, u32[]{:S(2)}) copy-start(f32[8,64,64]{2,1,0:T(8,128)} %param.19) | copy-start | bytes 393220
  84.3 13.7 %collective-permute-start.3 = (bf16[8,16,384]{2,1,0:T(8,128)(2,1)S(1)}, bf16[8,16,384]{2,1,0:T(8,128)(2,1)S(1)}, u32[]{:S(2)}, u32[]{:S(2)}) collective-permute-start(bf16[8,16,384]{2,1,0:T(8,128)(2,1)S(1)} %get-tuple-element.4), channel_id=1, source_target_pairs={{4,0},{8,4},{12,8},{16,12},{20,16},{24,20},{28,24},{0,28},{5,1},{9... | collective-permute-start | bytes 294920 | tf_op jit(solution)/shard_map/ppermute | solution.py:24
  85.7 12.3 %collective-permute-start.2 = (bf16[8,16,384]{2,1,0:T(8,128)(2,1)S(1)}, bf16[8,16,384]{2,1,0:T(8,128)(2,1)S(1)}, u32[]{:S(2)}, u32[]{:S(2)}) collective-permute-start(bf16[8,16,384]{2,1,0:T(8,128)(2,1)S(1)} %get-tuple-element.4), channel_id=1, source_target_pairs={{0,4},{4,8},{8,12},{12,16},{16,20},{20,24},{24,28},{28,0},{1,5},{5... | collective-permute-start | bytes 294920 | tf_op jit(solution)/shard_map/ppermute | solution.py:21
